TPU v7x, 256 devices: a whole 4x4x8 slice. The times are simulated.
256 devices in a mesh: grp: 32 (over x, z_hi, core), mem: 8 (over y, z_lo).
Axes of the slice: x: 4, y: 4, z: 8 (z_hi: 4, z_lo: 2; z = z_hi * 2 + z_lo), core: 2. Of those that a mesh axis runs over, the one named last changes fastest.
Arguments:
- forcing: float32 [16, 512, 128, 128], P(None, 'grp', 'mem'), may hold values from -8 to 8
- aggregate: int32 [128, 32, 32], P('grp', 'mem'), may hold values from 0 to 8191, as said below
- factors: float32 [64, 128, 128], P('mem'), may hold values from -1.5 to 1.5, as said below
Outputs:
- solution: float32 [16, 512, 128, 128], P(None, 'grp', 'mem')
Inputs may be any that keep to these rules, and one draw needn't show every extreme that they name: Coarse unknowns are numbered over the fine blocks with the first block index taken modulo half the number of blocks along the first dimension, consecutive numbers lying close together in the other dimensions, so that an aggregate joins blocks of both halves of the grid; a few blocks take the entry of a block beside them. `factors`: each of the 64 blocks is lower triangular with its diagonal between 0.5 and 1.5.
All inputs are finite; a program needn't handle non-finite values.
Results may differ from a plain program's by a relative error of at most 0.00013.
Values sent between devices are 32-bit elements; how exact they have to be, the bound alone decides.
No kernel may reach another device: no remote copies, remote signals or barrier semaphores. Data moves between devices by JAX's collectives and lax.ppermute only.
A program may use at most 128 MiB of HBM per device.

v0:
```python
import jax
import jax.numpy as jnp
from jax import lax
from jax.sharding import PartitionSpec as P

NC = 8192
PRE = 3
POST = 2


relaxation = 0.8


def with_halo(value, sides, width):
    edges = {}
    for axis, dim in sides:
        size, length = (lax.axis_size(axis), value.shape[dim])
        up = [(i, (i + 1) % size) for i in range(size - 1)]
        last = lax.slice_in_dim(value, length - width, length, axis=dim)
        initial = lax.slice_in_dim(value, 0, width, axis=dim)
        edges[dim] = (
            lax.ppermute(last, axis, up),
            lax.ppermute(initial, axis, [(b, a) for a, b in up]),
        )
    done = []
    for _, dim in sides:
        low, high = edges[dim]
        around = [(width, width) if d in done else (0, 0) for d in range(value.ndim)]
        value = jnp.concatenate([jnp.pad(low, around), value, jnp.pad(high, around)], axis=dim)
        done.append(dim)
    return value


def split_up(value, dim, size):
    before, after = (value.shape[:dim], value.shape[dim + 1 :])
    return jnp.moveaxis(value.reshape(*before, size, -1, *after), dim, 0)


def sum_at_owner(value, axis, dim):
    size = lax.axis_size(axis)
    pieces = lax.all_to_all(split_up(value, dim, size), axis, 0, 0, tiled=True)
    return jnp.sum(pieces, axis=0)


def from_everyone(value, axis):
    copies = jnp.broadcast_to(value, (lax.axis_size(axis), *value.shape))
    return lax.all_to_all(copies, axis, split_axis=0, concat_axis=0, tiled=True)


def of_everyone(value, axis):
    return from_everyone(value, axis).sum(axis=0)


def joined_along(pieces, dim):
    shape = list(pieces.shape[1:])
    shape[dim] *= pieces.shape[0]
    return jnp.moveaxis(pieces, 0, dim).reshape(shape)


def collect(value, axis, dim):
    pieces = from_everyone(value, axis)
    return joined_along(pieces, dim)


def stencil_inner(padded):
    centre = padded[:, 1:-1, 1:-1]
    beside = padded[:, 2:, 1:-1] + padded[:, :-2, 1:-1]
    beside = beside + padded[:, 1:-1, 2:] + padded[:, 1:-1, :-2]
    zeros_face = jnp.zeros(centre.shape[:3] + (1,), centre.dtype)
    upper_z = jnp.concatenate([centre[..., 1:], zeros_face], axis=3)
    lower_z = jnp.concatenate([zeros_face, centre[..., :-1]], axis=3)
    return 6.0 * centre - (beside + upper_z + lower_z)


def apply_operator(values):
    padded = with_halo(values, (("grp", 1), ("mem", 2)), 1)
    return stencil_inner(padded)


def restrict_blocks(residual, aggregate):
    blk_x, blk_y, blk_z = aggregate.shape
    sides = residual.shape[0]
    means = (
        residual.reshape(sides, blk_x, 4, blk_y, 4, blk_z, 4)
        .mean(axis=(2, 4, 6))
        .reshape(sides, -1)
    )
    summed = jax.ops.segment_sum(means.T, aggregate.reshape(-1), num_segments=NC)
    return summed.T


def prolong_blocks(coarse_fix, ids, valid):
    blk_x, blk_y, blk_z = ids.shape
    sides = coarse_fix.shape[0]
    picked = jnp.take(coarse_fix, ids.reshape(-1), axis=1) * valid.reshape(1, -1)
    picked = picked.reshape(sides, blk_x, 1, blk_y, 1, blk_z, 1)
    spread = jnp.broadcast_to(picked, (sides, blk_x, 4, blk_y, 4, blk_z, 4))
    return spread.reshape(sides, blk_x * 4, blk_y * 4, blk_z * 4)


def solve_blocks(coarse_rhs, factors):
    block_count = factors.shape[0]
    block_size = factors.shape[1]
    sides = coarse_rhs.shape[0]
    blocks = coarse_rhs.reshape(sides, block_count, block_size)
    inner = jnp.einsum("kbj,bij->kbi", blocks, factors, precision=lax.Precision.HIGHEST)
    result = jnp.einsum("kbi,bij->kbj", inner, factors, precision=lax.Precision.HIGHEST)
    return result.reshape(sides, block_count * block_size)


def shards(forcing, aggregate, factors):
    weight = relaxation / 6.0
    smoothed = weight * forcing
    for repeat in range(PRE - 1):
        smoothed = smoothed + weight * (forcing - apply_operator(smoothed))
    residual = forcing - apply_operator(smoothed)
    partial_value = restrict_blocks(residual, aggregate)
    shared = sum_at_owner(partial_value, "mem", 1)
    member_rhs = of_everyone(shared, "grp")
    coarse_fix = collect(solve_blocks(member_rhs, factors), "mem", 1)
    lifted = prolong_blocks(coarse_fix, aggregate, jnp.ones(aggregate.shape, jnp.float32))
    correction = lifted - weight * apply_operator(lifted)
    solution = smoothed + correction
    for repeat in range(POST):
        solution = solution + weight * (forcing - apply_operator(solution))
    return solution


def solution(mesh):
    placed = (P(None, "grp", "mem", None), P("grp", "mem", None), P("mem", None, None))
    return jax.shard_map(
        shards, mesh=mesh, in_specs=placed, out_specs=P(None, "grp", "mem", None), check_vma=False
    )
```

profile of v0, /device:TPU:1, one launch (start us, length us, event | category | flops | bytes accessed | tf_op | source)
XLA Modules:
  0.0 281.6 jit_solution(16892223736127361187)
XLA Ops:
  0.0 1.9 broadcast_multiply_fusion
  2.1 4.4 %collective-permute-start.3 = (f32[16,16,1,128]{3,1,2,0:T(8,128)S(1)}, f32[16,16,1,128]{3,1,2,0:T(8,128)S(1)}, u32[]{:S(2)}, u32[]{:S(2)}) collective-permute-start(f32[16,16,1,128]{3,1,2,0:T(8,128)S(1)} %bitcast.83), channel_id=1, source_target_pairs={{0,1},{1,2},{2,3},{3,4},{4,5},{5,6},{6,7},{8,9},{9,10},{10,11},{11... | collective-permute-start | bytes 393224 | tf_op jit(solution)/shard_map/ppermute | solution.py:22
  7.1 2.9 %collective-permute-start = (f32[16,1,16,128]{3,2,1,0:T(8,128)}, f32[16,1,16,128]{3,2,1,0:T(8,128)S(1)}, u32[]{:S(2)}, u32[]{:S(2)}) collective-permute-start(f32[16,1,16,128]{3,2,1,0:T(8,128)} %get-tuple-element.40), channel_id=1, source_target_pairs={{8,0},{16,8},{24,16},{32,24},{40,32},{48,40},{56,48},{64,56},{72,6... | collective-permute-start | bytes 393224 | tf_op jit(solution)/shard_map/ppermute | solution.py:23
  10.0 4.8 %collective-permute-start.1 = (f32[16,1,16,128]{3,2,1,0:T(8,128)S(1)}, f32[16,1,16,128]{3,2,1,0:T(8,128)S(1)}, u32[]{:S(2)}, u32[]{:S(2)}) collective-permute-start(f32[16,1,16,128]{3,2,1,0:T(8,128)S(1)} %get-tuple-element.39), channel_id=1, source_target_pairs={{0,8},{8,16},{16,24},{24,32},{32,40},{40,48},{48,56},{56,64},{64,7... | collective-permute-start | bytes 393224 | tf_op jit(solution)/shard_map/ppermute | solution.py:22
  16.3 2.7 fusion.83
  19.1 1.6 collective-permute-done.2
  20.7 6.8 %fusion.60 = f32[16,16,16,128]{3,2,1,0:T(8,128)S(1)} fusion(f32[16,16,16,128]{3,2,1,0:T(8,128)} %copy-done.5, f32[16,16,16,128]{3,2,1,0:T(8,128)S(1)} %copy-done.2, f32[16,16,1,128]{3,2,1,0:T(1,128)S(1)} %bitcast.67, f32[16,1,16,128]{3,2,1,0:T(8,128)S(1)} %collective-permute-done, f32[16,1,16,128]{3,2,1,0:T(8,128)S(1)} %collective-permute-done.1, ...), kind=kLoop, calls=%fused_computation.103 | loop fusion | flops 12582912 | bytes 10977280 | tf_op jit(solution)/shard_map/add | solution.py:115
  27.7 3.7 %collective-permute-start.7 = (f32[16,16,1,128]{3,1,2,0:T(8,128)S(1)}, f32[16,16,1,128]{3,1,2,0:T(8,128)S(1)}, u32[]{:S(2)}, u32[]{:S(2)}) collective-permute-start(f32[16,16,1,128]{3,1,2,0:T(8,128)S(1)} %bitcast.84), channel_id=1, source_target_pairs={{0,1},{1,2},{2,3},{3,4},{4,5},{5,6},{6,7},{8,9},{9,10},{10,11},{11... | collective-permute-start | bytes 393224 | tf_op jit(solution)/shard_map/ppermute | solution.py:22
  31.4 1.9 collective-permute-start.4
  33.3 5.6 %collective-permute-start.5 = (f32[16,1,16,128]{3,2,1,0:T(8,128)S(1)}, f32[16,1,16,128]{3,2,1,0:T(8,128)S(1)}, u32[]{:S(2)}, u32[]{:S(2)}) collective-permute-start(f32[16,1,16,128]{3,2,1,0:T(8,128)S(1)} %get-tuple-element.33), channel_id=1, source_target_pairs={{0,8},{8,16},{16,24},{24,32},{32,40},{40,48},{48,56},{56,64},{64,7... | collective-permute-start | bytes 393224 | tf_op jit(solution)/shard_map/ppermute | solution.py:22
  41.0 3.6 %collective-permute-done.6 = f32[16,16,1,128]{3,1,2,0:T(8,128)S(1)} collective-permute-done((f32[16,16,1,128]{3,1,2,0:T(8,128)S(1)}, f32[16,16,1,128]{3,1,2,0:T(8,128)S(1)}, u32[]{:S(2)}, u32[]{:S(2)}) %collective-permute-start.6) | collective-permute-done | bytes 131104 | tf_op jit(solution)/shard_map/ppermute | solution.py:23
  44.6 2.0 fusion.49
  46.8 3.5 %collective-permute-start.11 = (f32[16,16,1,128]{3,1,2,0:T(8,128)S(1)}, f32[16,16,1,128]{3,1,2,0:T(8,128)S(1)}, u32[]{:S(2)}, u32[]{:S(2)}) collective-permute-start(f32[16,16,1,128]{3,1,2,0:T(8,128)S(1)} %bitcast.85), channel_id=1, source_target_pairs={{0,1},{1,2},{2,3},{3,4},{4,5},{5,6},{6,7},{8,9},{9,10},{10,11},{11... | collective-permute-start | bytes 393224 | tf_op jit(solution)/shard_map/ppermute | solution.py:22
  50.3 1.9 collective-permute-start.8
  52.2 4.9 %collective-permute-start.9 = (f32[16,1,16,128]{3,2,1,0:T(8,128)S(1)}, f32[16,1,16,128]{3,2,1,0:T(8,128)S(1)}, u32[]{:S(2)}, u32[]{:S(2)}) collective-permute-start(f32[16,1,16,128]{3,2,1,0:T(8,128)S(1)} %get-tuple-element.27), channel_id=1, source_target_pairs={{0,8},{8,16},{16,24},{24,32},{32,40},{40,48},{48,56},{56,64},{64,7... | collective-permute-start | bytes 393224 | tf_op jit(solution)/shard_map/ppermute | solution.py:22
  59.2 3.6 %collective-permute-done.10 = f32[16,16,1,128]{3,1,2,0:T(8,128)S(1)} collective-permute-done((f32[16,16,1,128]{3,1,2,0:T(8,128)S(1)}, f32[16,16,1,128]{3,1,2,0:T(8,128)S(1)}, u32[]{:S(2)}, u32[]{:S(2)}) %collective-permute-start.10) | collective-permute-done | bytes 131104 | tf_op jit(solution)/shard_map/ppermute | solution.py:23
  62.8 2.9 %fusion.38 = f32[16,16,16,128]{3,2,1,0:T(8,128)} fusion(f32[16,16,16,128]{3,2,1,0:T(8,128)S(1)} %copy-done.2, f32[16,16,1,128]{3,2,1,0:T(1,128)S(1)} %bitcast.71, f32[16,1,16,128]{3,2,1,0:T(8,128)S(1)} %collective-permute-done.8, f32[16,16,16,128]{3,2,1,0:T(8,128)S(1)} %fusion.49, f32[16,1,16,128]{3,2,1,0:T(8,128)S(1)} %collective-permute-done.9, ...), kind=kLoop, calls=%fused_computation.65 | loop fusion | flops 11534336 | bytes 10977280 | tf_op jit(solution)/shard_map/sub | solution.py:116
  65.7 10.0 %copy.413 = f32[16,16,16,128]{0,3,2,1:T(8,128)} copy(f32[16,16,16,128]{3,2,1,0:T(8,128)} %fusion.38) | data formatting | bytes 4194304 | tf_op jit(solution)/shard_map/sub | solution.py:116
  75.7 9.4 %reduce_sum.27 = f32[16,4,4,32]{0,3,2,1:T(8,128)S(1)} reduce(f32[16,4,4,4,4,32,4]{0,6,5,4,3,2,1:T(4,128)} %bitcast.58, f32[]{:T(128)} %constant.11.clone.1), dimensions={2,4,6}, to_apply=%region_0.1 | reduce | flops 516096 | bytes 2129924 | tf_op jit(solution)/shard_map/reduce_sum | solution.py:85
  85.1 5.5 %scatter_custom_fusion = f32[8192,16]{1,0:T(8,128)} fusion(s32[512]{0:T(512)S(1)} %reshape.85, f32[512,16]{1,0:T(8,128)S(1)} %bitcast.65, f32[]{:T(128)} %constant.11.clone.1), kind=kCustom, calls=%fused_computation.116 | custom fusion | flops 8192 | bytes 524292 | tf_op jit(solution)/shard_map/scatter-add | solution.py:88
  90.6 2.8 copy.414
  93.4 14.0 %all_to_all.15 = f32[8,16,1024]{2,1,0:T(8,128)} all-to-all(f32[8,16,1024]{2,1,0:T(8,128)S(1)} %bitcast.62), channel_id=1, replica_groups=mesh['grp'=32,'mem'=8] {'mem'}, dimensions={0} | all-to-all | bytes 1048576 | tf_op jit(solution)/shard_map/all_to_all | solution.py:41
  108.8 63.7 %all_to_all.16 = f32[32,16,1024]{2,1,0:T(8,128)} all-to-all(f32[32,16,1024]{2,1,0:T(8,128)S(1)} %broadcast_in_dim.26), channel_id=1, replica_groups=mesh['grp'=32,'mem'=8] {'grp'}, dimensions={0} | all-to-all | bytes 4194304 | tf_op jit(solution)/shard_map/all_to_all | solution.py:47
  172.5 1.7 reduce_sum.29
  176.5 3.8 %all-to-all-start.2 = ((f32[8,16,1024]{2,1,0:T(8,128)}), f32[8,16,1024]{2,1,0:T(8,128)S(1)}, u32[]{:S(2)}, u32[]{:S(2)}) async-start(f32[8,16,1024]{2,1,0:T(8,128)} %broadcast_in_dim.27), calls=%async_computation.2 | async-start | bytes 1048576 | tf_op jit(solution)/shard_map/all_to_all | solution.py:47
  180.4 8.6 %all-to-all-done.2 = f32[8,16,1024]{2,1,0:T(8,128)S(1)} async-done(((f32[8,16,1024]{2,1,0:T(8,128)}), f32[8,16,1024]{2,1,0:T(8,128)S(1)}, u32[]{:S(2)}, u32[]{:S(2)}) %all-to-all-start.2) | async-done | bytes 524320 | tf_op jit(solution)/shard_map/all_to_all | solution.py:47
  189.0 2.6 copy.419
  191.6 3.2 %gather_fusion = f32[512,16]{1,0:T(8,128)S(1)} fusion(f32[16,8192]{0,1:T(8,128)} %bitcast.60, s32[1024]{0:T(1024)S(1)} %pad_clamp_fusion), kind=kCustom, calls=%fused_computation | custom fusion | bytes 67584 | tf_op jit(solution)/shard_map/jit(_take)/gather | solution.py:95
  195.0 6.3 %broadcast_in_dim.29 = f32[16,4,4,4,4,32,4]{0,6,5,4,3,2,1:T(4,128)} broadcast(f32[16,4,4,32]{0,3,2,1:T(8,128)S(1)} %broadcast_select_fusion), dimensions={0,1,3,5} | broadcast | bytes 2129920 | tf_op jit(solution)/shard_map/broadcast_in_dim | solution.py:97
  201.2 11.0 %copy.432 = f32[16,16,16,128]{3,2,1,0:T(8,128)} copy(f32[16,16,16,128]{0,3,2,1:T(8,128)} %bitcast.55) | data formatting | bytes 4194304 | tf_op jit(solution)/shard_map/reshape | solution.py:98
  212.3 3.1 %fusion.68 = (f32[16,16,1,128]{0,3,2,1:T(8,128)}, f32[16,16,1,128]{0,3,2,1:T(8,128)}) fusion(f32[16,16,16,128]{0,3,2,1:T(8,128)} %bitcast.56), kind=kLoop, calls=%fused_computation.130 | loop fusion | bytes 524288 | tf_op jit(solution)/shard_map/slice | solution.py:20
  215.4 3.1 %fusion.69 = (f32[16,1,16,128]{0,3,2,1:T(8,128)}, f32[16,1,16,128]{0,3,2,1:T(8,128)}) fusion(f32[16,16,16,128]{0,3,2,1:T(8,128)} %bitcast.57), kind=kLoop, calls=%fused_computation.131 | loop fusion | bytes 524288 | tf_op jit(solution)/shard_map/slice | solution.py:19
  220.1 2.3 collective-permute-start.15
  223.9 4.7 %collective-permute-start.12 = (f32[16,1,16,128]{3,2,1,0:T(8,128)S(1)}, f32[16,1,16,128]{3,2,1,0:T(8,128)S(1)}, u32[]{:S(2)}, u32[]{:S(2)}) collective-permute-start(f32[16,1,16,128]{3,2,1,0:T(8,128)S(1)} %copy.421), channel_id=1, source_target_pairs={{8,0},{16,8},{24,16},{32,24},{40,32},{48,40},{56,48},{64,56},{72,6... | collective-permute-start | bytes 393224 | tf_op jit(solution)/shard_map/ppermute | solution.py:23
  230.2 3.7 %collective-permute-start.13 = (f32[16,1,16,128]{3,2,1,0:T(8,128)S(1)}, f32[16,1,16,128]{3,2,1,0:T(8,128)S(1)}, u32[]{:S(2)}, u32[]{:S(2)}) collective-permute-start(f32[16,1,16,128]{3,2,1,0:T(8,128)S(1)} %copy.423), channel_id=1, source_target_pairs={{0,8},{8,16},{16,24},{24,32},{32,40},{40,48},{48,56},{56,64},{64,7... | collective-permute-start | bytes 393224 | tf_op jit(solution)/shard_map/ppermute | solution.py:22
  237.0 2.9 %fusion.76 = (f32[16,16,16,127]{3,2,1,0:T(8,128)S(1)}, f32[16,16,16,127]{3,2,1,0:T(8,128)S(1)}) fusion(f32[16,16,16,128]{3,2,1,0:T(8,128)} %copy.432), kind=kLoop, calls=%fused_computation.138 | loop fusion | bytes 8323072 | tf_op jit(solution)/shard_map/slice | solution.py:70
  240.0 2.0 collective-permute-done.14
  242.0 2.0 fusion.29
  244.3 3.3 %collective-permute-start.19 = (f32[16,16,1,128]{3,1,2,0:T(8,128)S(1)}, f32[16,16,1,128]{3,1,2,0:T(8,128)S(1)}, u32[]{:S(2)}, u32[]{:S(2)}) collective-permute-start(f32[16,16,1,128]{3,1,2,0:T(8,128)S(1)} %bitcast.86), channel_id=1, source_target_pairs={{0,1},{1,2},{2,3},{3,4},{4,5},{5,6},{6,7},{8,9},{9,10},{10,11},{11... | collective-permute-start | bytes 393224 | tf_op jit(solution)/shard_map/ppermute | solution.py:22
  247.6 2.3 collective-permute-start.16
  249.8 4.2 %collective-permute-start.17 = (f32[16,1,16,128]{3,2,1,0:T(8,128)S(1)}, f32[16,1,16,128]{3,2,1,0:T(8,128)S(1)}, u32[]{:S(2)}, u32[]{:S(2)}) collective-permute-start(f32[16,1,16,128]{3,2,1,0:T(8,128)S(1)} %get-tuple-element.19), channel_id=1, source_target_pairs={{0,8},{8,16},{16,24},{24,32},{32,40},{40,48},{48,56},{56,64},{64,7... | collective-permute-start | bytes 393224 | tf_op jit(solution)/shard_map/ppermute | solution.py:22
  256.1 3.7 %collective-permute-done.18 = f32[16,16,1,128]{3,1,2,0:T(8,128)S(1)} collective-permute-done((f32[16,16,1,128]{3,1,2,0:T(8,128)S(1)}, f32[16,16,1,128]{3,1,2,0:T(8,128)S(1)}, u32[]{:S(2)}, u32[]{:S(2)}) %collective-permute-start.18) | collective-permute-done | bytes 131104 | tf_op jit(solution)/shard_map/ppermute | solution.py:23
  259.8 2.0 fusion.18
  262.0 4.4 %collective-permute-start.23 = (f32[16,16,1,128]{3,1,2,0:T(8,128)S(1)}, f32[16,16,1,128]{3,1,2,0:T(8,128)S(1)}, u32[]{:S(2)}, u32[]{:S(2)}) collective-permute-start(f32[16,16,1,128]{3,1,2,0:T(8,128)S(1)} %bitcast.87), channel_id=1, source_target_pairs={{0,1},{1,2},{2,3},{3,4},{4,5},{5,6},{6,7},{8,9},{9,10},{10,11},{11... | collective-permute-start | bytes 393224 | tf_op jit(solution)/shard_map/ppermute | solution.py:22
  266.4 1.9 collective-permute-start.20
  268.4 4.5 %collective-permute-start.21 = (f32[16,1,16,128]{3,2,1,0:T(8,128)S(1)}, f32[16,1,16,128]{3,2,1,0:T(8,128)S(1)}, u32[]{:S(2)}, u32[]{:S(2)}) collective-permute-start(f32[16,1,16,128]{3,2,1,0:T(8,128)S(1)} %get-tuple-element.13), channel_id=1, source_target_pairs={{0,8},{8,16},{16,24},{24,32},{32,40},{40,48},{48,56},{56,64},{64,7... | collective-permute-start | bytes 393224 | tf_op jit(solution)/shard_map/ppermute | solution.py:22
  275.0 3.6 %collective-permute-done.22 = f32[16,16,1,128]{3,1,2,0:T(8,128)S(1)} collective-permute-done((f32[16,16,1,128]{3,1,2,0:T(8,128)S(1)}, f32[16,16,1,128]{3,1,2,0:T(8,128)S(1)}, u32[]{:S(2)}, u32[]{:S(2)}) %collective-permute-start.22) | collective-permute-done | bytes 131104 | tf_op jit(solution)/shard_map/ppermute | solution.py:23
  278.6 2.9 %fusion.7 = f32[16,16,16,128]{3,2,1,0:T(8,128)} fusion(f32[16,16,16,128]{3,2,1,0:T(8,128)S(1)} %fusion.18, f32[16,16,16,128]{3,2,1,0:T(8,128)S(1)} %copy-done.2, f32[16,16,1,128]{3,2,1,0:T(1,128)S(1)} %bitcast.70, f32[16,1,16,128]{3,2,1,0:T(8,128)S(1)} %collective-permute-done.20, f32[16,1,16,128]{3,2,1,0:T(8,128)S(1)} %collective-permute-done.21, ...), kind=kLoop, calls=%fused_computation.10 | loop fusion | flops 12582912 | bytes 10977280 | tf_op jit(solution)/shard_map/add | solution.py:125
  (71 shorter events, 23.1 us)
Async XLA Ops:
  0.0 174.2 %copy-start = (f32[8,128,128]{2,1,0:T(8,128)S(1)}, f32[8,128,128]{2,1,0:T(8,128)}, u32[]{:S(2)}) copy-start(f32[8,128,128]{2,1,0:T(8,128)} %param.5) | copy-start | bytes 1572868
  1.9 14.4 %copy-start.5 = (f32[16,16,16,128]{3,2,1,0:T(8,128)}, f32[16,16,16,128]{3,2,1,0:T(8,128)S(1)}, u32[]{:S(2)}) copy-start(f32[16,16,16,128]{3,2,1,0:T(8,128)S(1)} %broadcast_multiply_fusion) | copy-start | bytes 6291460
  2.1 17.0 %collective-permute-start.3 = (f32[16,16,1,128]{3,1,2,0:T(8,128)S(1)}, f32[16,16,1,128]{3,1,2,0:T(8,128)S(1)}, u32[]{:S(2)}, u32[]{:S(2)}) collective-permute-start(f32[16,16,1,128]{3,1,2,0:T(8,128)S(1)} %bitcast.83), channel_id=1, source_target_pairs={{0,1},{1,2},{2,3},{3,4},{4,5},{5,6},{6,7},{8,9},{9,10},{10,11},{11... | collective-permute-start | bytes 393224 | tf_op jit(solution)/shard_map/ppermute | solution.py:22
  7.1 11.9 %collective-permute-start = (f32[16,1,16,128]{3,2,1,0:T(8,128)}, f32[16,1,16,128]{3,2,1,0:T(8,128)S(1)}, u32[]{:S(2)}, u32[]{:S(2)}) collective-permute-start(f32[16,1,16,128]{3,2,1,0:T(8,128)} %get-tuple-element.40), channel_id=1, source_target_pairs={{8,0},{16,8},{24,16},{32,24},{40,32},{48,40},{56,48},{64,56},{72,6... | collective-permute-start | bytes 393224 | tf_op jit(solution)/shard_map/ppermute | solution.py:23
  10.0 9.1 %collective-permute-start.1 = (f32[16,1,16,128]{3,2,1,0:T(8,128)S(1)}, f32[16,1,16,128]{3,2,1,0:T(8,128)S(1)}, u32[]{:S(2)}, u32[]{:S(2)}) collective-permute-start(f32[16,1,16,128]{3,2,1,0:T(8,128)S(1)} %get-tuple-element.39), channel_id=1, source_target_pairs={{0,8},{8,16},{16,24},{24,32},{32,40},{40,48},{48,56},{56,64},{64,7... | collective-permute-start | bytes 393224 | tf_op jit(solution)/shard_map/ppermute | solution.py:22
  14.8 4.2 %copy-start.7 = (s32[4,4,32]{2,1,0:T(4,128)S(1)}, s32[4,4,32]{2,1,0:T(4,128)}, u32[]{:S(2)}) copy-start(s32[4,4,32]{2,1,0:T(4,128)} %param.4) | copy-start | bytes 6148
  14.8 5.9 %copy-start.2 = (f32[16,16,16,128]{3,2,1,0:T(8,128)S(1)}, f32[16,16,16,128]{3,2,1,0:T(8,128)}, u32[]{:S(2)}) copy-start(f32[16,16,16,128]{3,2,1,0:T(8,128)} %param.3) | copy-start | bytes 6291460
  14.8 5.8 %collective-permute-start.2 = (f32[16,16,1,128]{3,1,2,0:T(8,128)S(1)}, f32[16,16,1,128]{3,1,2,0:T(8,128)S(1)}, u32[]{:S(2)}, u32[]{:S(2)}) collective-permute-start(f32[16,16,1,128]{3,1,2,0:T(8,128)S(1)} %bitcast.78), channel_id=1, source_target_pairs={{1,0},{2,1},{3,2},{4,3},{5,4},{6,5},{7,6},{9,8},{10,9},{11,10},{12... | collective-permute-start | bytes 393224 | tf_op jit(solution)/shard_map/ppermute | solution.py:23
  27.7 13.2 %collective-permute-start.7 = (f32[16,16,1,128]{3,1,2,0:T(8,128)S(1)}, f32[16,16,1,128]{3,1,2,0:T(8,128)S(1)}, u32[]{:S(2)}, u32[]{:S(2)}) collective-permute-start(f32[16,16,1,128]{3,1,2,0:T(8,128)S(1)} %bitcast.84), channel_id=1, source_target_pairs={{0,1},{1,2},{2,3},{3,4},{4,5},{5,6},{6,7},{8,9},{9,10},{10,11},{11... | collective-permute-start | bytes 393224 | tf_op jit(solution)/shard_map/ppermute | solution.py:22
  31.4 9.6 %collective-permute-start.4 = (f32[16,1,16,128]{3,2,1,0:T(8,128)S(1)}, f32[16,1,16,128]{3,2,1,0:T(8,128)S(1)}, u32[]{:S(2)}, u32[]{:S(2)}) collective-permute-start(f32[16,1,16,128]{3,2,1,0:T(8,128)S(1)} %get-tuple-element.34), channel_id=1, source_target_pairs={{8,0},{16,8},{24,16},{32,24},{40,32},{48,40},{56,48},{64,56},{72,6... | collective-permute-start | bytes 393224 | tf_op jit(solution)/shard_map/ppermute | solution.py:23
  33.3 7.6 %collective-permute-start.5 = (f32[16,1,16,128]{3,2,1,0:T(8,128)S(1)}, f32[16,1,16,128]{3,2,1,0:T(8,128)S(1)}, u32[]{:S(2)}, u32[]{:S(2)}) collective-permute-start(f32[16,1,16,128]{3,2,1,0:T(8,128)S(1)} %get-tuple-element.33), channel_id=1, source_target_pairs={{0,8},{8,16},{16,24},{24,32},{32,40},{40,48},{48,56},{56,64},{64,7... | collective-permute-start | bytes 393224 | tf_op jit(solution)/shard_map/ppermute | solution.py:22
  38.9 5.7 %collective-permute-start.6 = (f32[16,16,1,128]{3,1,2,0:T(8,128)S(1)}, f32[16,16,1,128]{3,1,2,0:T(8,128)S(1)}, u32[]{:S(2)}, u32[]{:S(2)}) collective-permute-start(f32[16,16,1,128]{3,1,2,0:T(8,128)S(1)} %bitcast.79), channel_id=1, source_target_pairs={{1,0},{2,1},{3,2},{4,3},{5,4},{6,5},{7,6},{9,8},{10,9},{11,10},{12... | collective-permute-start | bytes 393224 | tf_op jit(solution)/shard_map/ppermute | solution.py:23
  46.6 16.3 %copy-start.3 = (f32[16,16,16,128]{3,2,1,0:T(8,128)}, f32[16,16,16,128]{3,2,1,0:T(8,128)S(1)}, u32[]{:S(2)}) copy-start(f32[16,16,16,128]{3,2,1,0:T(8,128)S(1)} %fusion.49) | copy-start | bytes 6291460
  46.8 12.4 %collective-permute-start.11 = (f32[16,16,1,128]{3,1,2,0:T(8,128)S(1)}, f32[16,16,1,128]{3,1,2,0:T(8,128)S(1)}, u32[]{:S(2)}, u32[]{:S(2)}) collective-permute-start(f32[16,16,1,128]{3,1,2,0:T(8,128)S(1)} %bitcast.85), channel_id=1, source_target_pairs={{0,1},{1,2},{2,3},{3,4},{4,5},{5,6},{6,7},{8,9},{9,10},{10,11},{11... | collective-permute-start | bytes 393224 | tf_op jit(solution)/shard_map/ppermute | solution.py:22
  50.3 8.9 %collective-permute-start.8 = (f32[16,1,16,128]{3,2,1,0:T(8,128)S(1)}, f32[16,1,16,128]{3,2,1,0:T(8,128)S(1)}, u32[]{:S(2)}, u32[]{:S(2)}) collective-permute-start(f32[16,1,16,128]{3,2,1,0:T(8,128)S(1)} %get-tuple-element.28), channel_id=1, source_target_pairs={{8,0},{16,8},{24,16},{32,24},{40,32},{48,40},{56,48},{64,56},{72,6... | collective-permute-start | bytes 393224 | tf_op jit(solution)/shard_map/ppermute | solution.py:23
  52.2 7.0 %collective-permute-start.9 = (f32[16,1,16,128]{3,2,1,0:T(8,128)S(1)}, f32[16,1,16,128]{3,2,1,0:T(8,128)S(1)}, u32[]{:S(2)}, u32[]{:S(2)}) collective-permute-start(f32[16,1,16,128]{3,2,1,0:T(8,128)S(1)} %get-tuple-element.27), channel_id=1, source_target_pairs={{0,8},{8,16},{16,24},{24,32},{32,40},{40,48},{48,56},{56,64},{64,7... | collective-permute-start | bytes 393224 | tf_op jit(solution)/shard_map/ppermute | solution.py:22
  57.1 5.7 %collective-permute-start.10 = (f32[16,16,1,128]{3,1,2,0:T(8,128)S(1)}, f32[16,16,1,128]{3,1,2,0:T(8,128)S(1)}, u32[]{:S(2)}, u32[]{:S(2)}) collective-permute-start(f32[16,16,1,128]{3,1,2,0:T(8,128)S(1)} %bitcast.80), channel_id=1, source_target_pairs={{1,0},{2,1},{3,2},{4,3},{5,4},{6,5},{7,6},{9,8},{10,9},{11,10},{12... | collective-permute-start | bytes 393224 | tf_op jit(solution)/shard_map/ppermute | solution.py:23
  176.5 12.5 %all-to-all-start.2 = ((f32[8,16,1024]{2,1,0:T(8,128)}), f32[8,16,1024]{2,1,0:T(8,128)S(1)}, u32[]{:S(2)}, u32[]{:S(2)}) async-start(f32[8,16,1024]{2,1,0:T(8,128)} %broadcast_in_dim.27), calls=%async_computation.2 | async-start | bytes 1048576 | tf_op jit(solution)/shard_map/all_to_all | solution.py:47
  220.1 19.9 %collective-permute-start.15 = (f32[16,16,1,128]{3,1,2,0:T(8,128)S(1)}, f32[16,16,1,128]{3,1,2,0:T(8,128)S(1)}, u32[]{:S(2)}, u32[]{:S(2)}) collective-permute-start(f32[16,16,1,128]{3,1,2,0:T(8,128)S(1)} %copy.428), channel_id=1, source_target_pairs={{0,1},{1,2},{2,3},{3,4},{4,5},{5,6},{6,7},{8,9},{9,10},{10,11},{11... | collective-permute-start | bytes 393224 | tf_op jit(solution)/shard_map/ppermute | solution.py:22
  223.9 16.1 %collective-permute-start.12 = (f32[16,1,16,128]{3,2,1,0:T(8,128)S(1)}, f32[16,1,16,128]{3,2,1,0:T(8,128)S(1)}, u32[]{:S(2)}, u32[]{:S(2)}) collective-permute-start(f32[16,1,16,128]{3,2,1,0:T(8,128)S(1)} %copy.421), channel_id=1, source_target_pairs={{8,0},{16,8},{24,16},{32,24},{40,32},{48,40},{56,48},{64,56},{72,6... | collective-permute-start | bytes 393224 | tf_op jit(solution)/shard_map/ppermute | solution.py:23
  230.2 9.8 %collective-permute-start.13 = (f32[16,1,16,128]{3,2,1,0:T(8,128)S(1)}, f32[16,1,16,128]{3,2,1,0:T(8,128)S(1)}, u32[]{:S(2)}, u32[]{:S(2)}) collective-permute-start(f32[16,1,16,128]{3,2,1,0:T(8,128)S(1)} %copy.423), channel_id=1, source_target_pairs={{0,8},{8,16},{16,24},{24,32},{32,40},{40,48},{48,56},{56,64},{64,7... | collective-permute-start | bytes 393224 | tf_op jit(solution)/shard_map/ppermute | solution.py:22
  235.4 6.6 %copy-start.4 = (f32[16,16,16,128]{3,2,1,0:T(8,128)S(1)}, f32[16,16,16,128]{3,2,1,0:T(8,128)}, u32[]{:S(2)}) copy-start(f32[16,16,16,128]{3,2,1,0:T(8,128)} %copy-done.3) | copy-start | bytes 6291460
  235.4 6.6 %copy-start.6 = (f32[16,16,16,128]{3,2,1,0:T(8,128)S(1)}, f32[16,16,16,128]{3,2,1,0:T(8,128)}, u32[]{:S(2)}) copy-start(f32[16,16,16,128]{3,2,1,0:T(8,128)} %copy.432) | copy-start | bytes 6291460
  235.4 6.6 %collective-permute-start.14 = (f32[16,16,1,128]{3,1,2,0:T(8,128)S(1)}, f32[16,16,1,128]{3,1,2,0:T(8,128)S(1)}, u32[]{:S(2)}, u32[]{:S(2)}) collective-permute-start(f32[16,16,1,128]{3,1,2,0:T(8,128)S(1)} %copy.426), channel_id=1, source_target_pairs={{1,0},{2,1},{3,2},{4,3},{5,4},{6,5},{7,6},{9,8},{10,9},{11,10},{12... | collective-permute-start | bytes 393224 | tf_op jit(solution)/shard_map/ppermute | solution.py:23
  244.3 11.8 %collective-permute-start.19 = (f32[16,16,1,128]{3,1,2,0:T(8,128)S(1)}, f32[16,16,1,128]{3,1,2,0:T(8,128)S(1)}, u32[]{:S(2)}, u32[]{:S(2)}) collective-permute-start(f32[16,16,1,128]{3,1,2,0:T(8,128)S(1)} %bitcast.86), channel_id=1, source_target_pairs={{0,1},{1,2},{2,3},{3,4},{4,5},{5,6},{6,7},{8,9},{9,10},{10,11},{11... | collective-permute-start | bytes 393224 | tf_op jit(solution)/shard_map/ppermute | solution.py:22
  247.6 8.5 %collective-permute-start.16 = (f32[16,1,16,128]{3,2,1,0:T(8,128)S(1)}, f32[16,1,16,128]{3,2,1,0:T(8,128)S(1)}, u32[]{:S(2)}, u32[]{:S(2)}) collective-permute-start(f32[16,1,16,128]{3,2,1,0:T(8,128)S(1)} %get-tuple-element.20), channel_id=1, source_target_pairs={{8,0},{16,8},{24,16},{32,24},{40,32},{48,40},{56,48},{64,56},{72,6... | collective-permute-start | bytes 393224 | tf_op jit(solution)/shard_map/ppermute | solution.py:23
  249.8 6.3 %collective-permute-start.17 = (f32[16,1,16,128]{3,2,1,0:T(8,128)S(1)}, f32[16,1,16,128]{3,2,1,0:T(8,128)S(1)}, u32[]{:S(2)}, u32[]{:S(2)}) collective-permute-start(f32[16,1,16,128]{3,2,1,0:T(8,128)S(1)} %get-tuple-element.19), channel_id=1, source_target_pairs={{0,8},{8,16},{16,24},{24,32},{32,40},{40,48},{48,56},{56,64},{64,7... | collective-permute-start | bytes 393224 | tf_op jit(solution)/shard_map/ppermute | solution.py:22
  254.0 5.8 %collective-permute-start.18 = (f32[16,16,1,128]{3,1,2,0:T(8,128)S(1)}, f32[16,16,1,128]{3,1,2,0:T(8,128)S(1)}, u32[]{:S(2)}, u32[]{:S(2)}) collective-permute-start(f32[16,16,1,128]{3,1,2,0:T(8,128)S(1)} %bitcast.81), channel_id=1, source_target_pairs={{1,0},{2,1},{3,2},{4,3},{5,4},{6,5},{7,6},{9,8},{10,9},{11,10},{12... | collective-permute-start | bytes 393224 | tf_op jit(solution)/shard_map/ppermute | solution.py:23
  262.0 12.9 %collective-permute-start.23 = (f32[16,16,1,128]{3,1,2,0:T(8,128)S(1)}, f32[16,16,1,128]{3,1,2,0:T(8,128)S(1)}, u32[]{:S(2)}, u32[]{:S(2)}) collective-permute-start(f32[16,16,1,128]{3,1,2,0:T(8,128)S(1)} %bitcast.87), channel_id=1, source_target_pairs={{0,1},{1,2},{2,3},{3,4},{4,5},{5,6},{6,7},{8,9},{9,10},{10,11},{11... | collective-permute-start | bytes 393224 | tf_op jit(solution)/shard_map/ppermute | solution.py:22
  266.4 8.5 %collective-permute-start.20 = (f32[16,1,16,128]{3,2,1,0:T(8,128)S(1)}, f32[16,1,16,128]{3,2,1,0:T(8,128)S(1)}, u32[]{:S(2)}, u32[]{:S(2)}) collective-permute-start(f32[16,1,16,128]{3,2,1,0:T(8,128)S(1)} %get-tuple-element.14), channel_id=1, source_target_pairs={{8,0},{16,8},{24,16},{32,24},{40,32},{48,40},{56,48},{64,56},{72,6... | collective-permute-start | bytes 393224 | tf_op jit(solution)/shard_map/ppermute | solution.py:23
  268.4 6.6 %collective-permute-start.21 = (f32[16,1,16,128]{3,2,1,0:T(8,128)S(1)}, f32[16,1,16,128]{3,2,1,0:T(8,128)S(1)}, u32[]{:S(2)}, u32[]{:S(2)}) collective-permute-start(f32[16,1,16,128]{3,2,1,0:T(8,128)S(1)} %get-tuple-element.13), channel_id=1, source_target_pairs={{0,8},{8,16},{16,24},{24,32},{32,40},{40,48},{48,56},{56,64},{64,7... | collective-permute-start | bytes 393224 | tf_op jit(solution)/shard_map/ppermute | solution.py:22
  272.9 5.7 %collective-permute-start.22 = (f32[16,16,1,128]{3,1,2,0:T(8,128)S(1)}, f32[16,16,1,128]{3,1,2,0:T(8,128)S(1)}, u32[]{:S(2)}, u32[]{:S(2)}) collective-permute-start(f32[16,16,1,128]{3,1,2,0:T(8,128)S(1)} %bitcast.82), channel_id=1, source_target_pairs={{1,0},{2,1},{3,2},{4,3},{5,4},{6,5},{7,6},{9,8},{10,9},{11,10},{12... | collective-permute-start | bytes 393224 | tf_op jit(solution)/shard_map/ppermute | solution.py:23
  278.6 2.9 %copy-start.1 = (f32[8,128,128]{2,1,0:T(8,128)S(1)}, f32[8,128,128]{2,1,0:T(8,128)}, u32[]{:S(2)}) copy-start(f32[8,128,128]{2,1,0:T(8,128)} %param.5) | copy-start | bytes 1572868
where the time goes:
time: 285 us; the launch traced here: 282 us
  blocking collectives  77.7 us (27%)
  starting transfers between devices  76.7 us (27%)
  local copies, waits for them, and re-layouts  59.9 us (21%)
  other arithmetic  38.3 us (13%)
  waiting for transfers between devices  26.8 us (9%)
    all_to_all x1, blocking collectives, from_everyone(): return lax.all_to_all(copies, axis, split_axis=0, concat_axis=0, tiled=True)  63.7 us
    ppermute x12, starting transfers between devices, with_halo(): lax.ppermute(last, axis, up)  49.2 us
    ppermute x12, starting transfers between devices, with_halo(): lax.ppermute(initial, axis, [(b, a) for a, b in up])  23.8 us
    ppermute x12, waiting for transfers between devices, with_halo(): lax.ppermute(initial, axis, [(b, a) for a, b in up])  18.2 us
    all_to_all x1, blocking collectives, sum_at_owner(): pieces = lax.all_to_all(split_up(value, dim, size), axis, 0, 0, tiled=True)  14 us
    reshape x1, local copies, waits for them, and re-layouts, prolong_blocks(): return spread.reshape(sides, blk_x * 4, blk_y * 4, blk_z * 4)  11 us
    sub x1, local copies, waits for them, and re-layouts, shards(): residual = forcing - apply_operator(smoothed)  10 us
    reduce_sum x1, other arithmetic, restrict_blocks(): means = residual.reshape(sides, blk_x, 4, blk_y, 4, blk_z, 4).mean(axis=(...  9.37 us
  transfers between devices with their start and end apart: 25, of which 7 were waited for; matrix products, arithmetic and copies ran while one was open for 5% of the time, Pallas kernels for 0%

commit v1 on v0

v1 whole, which is shorter than its diff:
```python
import functools
import math

import jax
import jax.numpy as jnp
import numpy as np
from jax import lax
from jax.experimental import pallas as pl
from jax.experimental.pallas import tpu as pltpu
from jax.sharding import PartitionSpec as P

NC = 8192
RHS = 16
BS = 128
SIDE = 16
NZ = 128
RIM = 4
WIDE = SIDE + 2 * RIM
BLK = WIDE // 4
NBLK = BLK * BLK
WEIGHT = 0.8 / 6.0
BOTH = ("grp", "mem")
F32, BF16 = jnp.float32, jnp.bfloat16


def line_operator(size):
    return (
        (1.0 / 3.0 - 2.0 * WEIGHT) * np.eye(size)
        + WEIGHT * np.eye(size, k=1)
        + WEIGHT * np.eye(size, k=-1)
    )


def block_sums(size):
    return np.kron(np.eye(size // 4), np.ones((1, 4)))


def side_tables():
    out = np.zeros((3, 4, BLK, SIDE))
    for place in range(3):
        keep = np.ones(WIDE)
        if place == 1:
            keep[:RIM] = 0
        if place == 2:
            keep[-RIM:] = 0
        step = line_operator(WIDE) * keep[:, None] * keep[None, :]
        power = np.diag(keep)
        for p in range(4):
            out[place, p] = (block_sums(WIDE) @ power)[:, RIM:-RIM]
            power = power @ step
    return out


def split_const(value):
    value = np.asarray(value, np.float32)
    high = value.astype(jnp.bfloat16)
    low = (value - high.astype(np.float32)).astype(jnp.bfloat16)
    return np.stack([high, low])


@functools.cache
def tables():
    side = side_tables()
    plane = np.zeros((3, 3, 4, NBLK, SIDE * SIDE))
    for j in range(4):
        for p in range(4 - j):
            q = 3 - j - p
            factor = 6.0 / (math.factorial(p) * math.factorial(q) * math.factorial(j)) / 64.0
            plane[:, :, j] += factor * np.einsum("aXx,bYy->abXYxy", side[:, p], side[:, q]).reshape(
                3, 3, NBLK, SIDE * SIDE
            )
    plane = split_const(plane.reshape(9, 4 * NBLK, SIDE * SIDE)).transpose(1, 0, 2, 3)
    power = np.eye(NZ)
    lines = []
    for j in range(4):
        lines.append(power @ block_sums(NZ).T)
        power = power @ line_operator(NZ)
    lines = np.stack(lines)
    gather_z = np.tile(lines.reshape(4 * NZ, NZ // 4), (1, 4))
    spread_z = 64.0 * np.tile(lines.transpose(2, 0, 1).reshape(NZ // 4, 4 * NZ), (4, 1))
    return plane, split_const(gather_z), split_const(spread_z)


def split(value):
    high = value.astype(BF16)
    return high, (value - high.astype(F32)).astype(BF16)


def dot(a, b, dims=(((1,), (0,)), ((), ()))):
    return lax.dot_general(a, b, dims, preferred_element_type=F32)


def dot3(a, b, dims=(((1,), (0,)), ((), ()))):
    return dot(a[0], b[0], dims) + dot(a[0], b[1], dims) + dot(a[1], b[0], dims)


GROUPS = NBLK // 4


def slot_lanes(rows):
    return lax.broadcasted_iota(jnp.int32, (rows, NZ), 1) // (NZ // 4)


def restrict_kernel(place_ref, f_ref, plane_ref, line_ref, out_ref, part_ref):
    plane = (plane_ref[0, 0], plane_ref[0, 1])
    for k in range(0, RHS, 2):
        pair = [f_ref[k + i].reshape(SIDE * SIDE, NZ) for i in range(2)]
        value = dot3(plane, split(jnp.concatenate(pair, axis=1)))
        for i in range(2):
            part_ref[pl.ds(k + i, 4 * NBLK, stride=RHS), :] = value[:, i * NZ : (i + 1) * NZ]
    line = (line_ref[0], line_ref[1])
    slots = slot_lanes(GROUPS * RHS)
    total = jnp.zeros((GROUPS * RHS, NZ), F32)
    for s in range(4):
        columns = []
        for j in range(4):
            rows = [
                part_ref[pl.ds((j * NBLK + g * 4 + s) * RHS, RHS), :] for g in range(GROUPS)
            ]
            columns.append(jnp.concatenate(rows, axis=0))
        value = dot3(split(jnp.concatenate(columns, axis=1)), line)
        total = jnp.where(slots == s, value, total)
    out_ref[...] = total


def full(shape):
    return pl.BlockSpec(shape, lambda i, place: (0,) * len(shape))


def restrict_own(forcing, place):
    plane, gather_z, _ = tables()
    return pl.pallas_call(
        restrict_kernel,
        out_shape=jax.ShapeDtypeStruct((GROUPS * RHS, NZ), F32),
        grid_spec=pltpu.PrefetchScalarGridSpec(
            num_scalar_prefetch=1,
            grid=(1,),
            in_specs=[
                full(forcing.shape),
                pl.BlockSpec((1,) + plane.shape[1:], lambda i, place: (place[0], 0, 0, 0)),
                full(gather_z.shape),
            ],
            out_specs=full((GROUPS * RHS, NZ)),
            scratch_shapes=[pltpu.VMEM((4 * NBLK * RHS, NZ), F32)],
        ),
        cost_estimate=pl.CostEstimate(
            flops=6 * 10**9, bytes_accessed=3 * 2**20, transcendentals=0
        ),
        name="restrict",
    )(place, forcing, jnp.asarray(plane), jnp.asarray(gather_z))


def correct_kernel(place_ref, c_ref, q_ref, plane_ref, line_ref, out_ref, part_ref):
    value = c_ref[...]
    line = (line_ref[0], line_ref[1])
    slots = slot_lanes(GROUPS * RHS)
    for s in range(4):
        spread = dot3(split(jnp.where(slots == s, value, 0.0)), line)
        for j in range(4):
            for g in range(GROUPS):
                part_ref[pl.ds((j * NBLK + g * 4 + s) * RHS, RHS), :] = spread[
                    g * RHS : (g + 1) * RHS, j * NZ : (j + 1) * NZ
                ]
    plane = (plane_ref[0, 0], plane_ref[0, 1])
    for k in range(0, RHS, 2):
        pair = [part_ref[pl.ds(k + i, 4 * NBLK, stride=RHS), :] for i in range(2)]
        value = dot3(plane, split(jnp.concatenate(pair, axis=1)), (((0,), (0,)), ((), ())))
        for i in range(2):
            own = value[:, i * NZ : (i + 1) * NZ].reshape(SIDE, SIDE, NZ)
            out_ref[k + i] = q_ref[k + i] + own


def add_correction(smooth, coarse, place):
    plane, _, spread_z = tables()
    return pl.pallas_call(
        correct_kernel,
        out_shape=jax.ShapeDtypeStruct(smooth.shape, F32),
        grid_spec=pltpu.PrefetchScalarGridSpec(
            num_scalar_prefetch=1,
            grid=(1,),
            in_specs=[
                full(coarse.shape),
                full(smooth.shape),
                pl.BlockSpec((1,) + plane.shape[1:], lambda i, place: (place[0], 0, 0, 0)),
                full(spread_z.shape),
            ],
            out_specs=full(smooth.shape),
            scratch_shapes=[pltpu.VMEM((4 * NBLK * RHS, NZ), F32)],
        ),
        cost_estimate=pl.CostEstimate(
            flops=6 * 10**9, bytes_accessed=5 * 2**20, transcendentals=0
        ),
        name="correct",
    )(place, coarse, smooth, jnp.asarray(plane), jnp.asarray(spread_z))


SWEEPS = 4


def smooth_kernel(inside_ref, f_ref, ylo_ref, yhi_ref, xlo_ref, xhi_ref, out_ref, src, one, two):
    low_x, high_x = inside_ref[0], inside_ref[1]
    row = lax.broadcasted_iota(jnp.int32, (WIDE, NZ), 0)
    low_y = jnp.where(row < RIM, inside_ref[2].astype(F32), 1.0)
    in_y = jnp.where(row >= RIM + SIDE, inside_ref[3].astype(F32), low_y)
    lane = lax.broadcasted_iota(jnp.int32, (WIDE, NZ), 1)
    has_lower, has_upper = lane > 0, lane < NZ - 1

    def load(k):
        for x in range(RIM):
            src[x] = xlo_ref[k, x]
            src[RIM + SIDE + x] = xhi_ref[k, x]
        for x in range(SIDE):
            src[RIM + x, pl.ds(0, RIM), :] = ylo_ref[k, x]
            src[RIM + x, pl.ds(RIM, SIDE), :] = f_ref[k, x]
            src[RIM + x, pl.ds(RIM + SIDE, RIM), :] = yhi_ref[k, x]
        for x in range(WIDE):
            value = WEIGHT * src[x]
            src[x] = value
            one[x] = value

    def sweep(t, old, new, k):
        for x in range(t, WIDE - t):
            here = old[x]
            near = old[x - 1] + old[x + 1]
            near += pltpu.roll(here, 1, 0) + pltpu.roll(here, WIDE - 1, 0)
            near += jnp.where(has_lower, pltpu.roll(here, 1, 1), 0.0)
            near += jnp.where(has_upper, pltpu.roll(here, NZ - 1, 1), 0.0)
            value = src[x] + (1.0 - 6.0 * WEIGHT) * here + WEIGHT * near
            if t == SWEEPS:
                out_ref[k, x - RIM] = value[RIM : RIM + SIDE]
                continue
            value = value * in_y
            if x < RIM:
                value = value * low_x.astype(F32)
            if x >= RIM + SIDE:
                value = value * high_x.astype(F32)
            new[x] = value

    def body(k, carry):
        load(k)
        bufs = (one, two)
        for t in range(1, SWEEPS + 1):
            sweep(t, bufs[(t - 1) % 2], bufs[t % 2], k)
        return carry

    lax.fori_loop(0, f_ref.shape[0], body, 0)


def smooth_all(forcing, ylo, yhi, xlo, xhi, inside):
    steps = 4
    each = RHS // steps

    def part(value):
        return pl.BlockSpec((each,) + value.shape[1:], lambda i, place: (i, 0, 0, 0))

    args = (forcing, ylo, yhi, xlo, xhi)
    return pl.pallas_call(
        smooth_kernel,
        out_shape=jax.ShapeDtypeStruct(forcing.shape, F32),
        grid_spec=pltpu.PrefetchScalarGridSpec(
            num_scalar_prefetch=1,
            grid=(steps,),
            in_specs=[part(a) for a in args],
            out_specs=part(forcing),
            scratch_shapes=[pltpu.VMEM((WIDE, WIDE, NZ), F32)] * 3,
        ),
        cost_estimate=pl.CostEstimate(
            flops=10**10, bytes_accessed=7 * 2**20, transcendentals=0
        ),
        name="smooth",
    )(inside, *args)


def shift_pairs(size):
    up = [(i, i + 1) for i in range(size - 1)]
    return up, [(b, a) for a, b in up]


def rim_of(value, axis, dim, width):
    size, length = lax.axis_size(axis), value.shape[dim]
    up, down = shift_pairs(size)
    low = lax.ppermute(lax.slice_in_dim(value, length - width, length, axis=dim), axis, up)
    high = lax.ppermute(lax.slice_in_dim(value, 0, width, axis=dim), axis, down)
    return low, high


def with_rim(value, axis, dim, width):
    low, high = rim_of(value, axis, dim, width)
    return jnp.concatenate([low, value, high], axis=dim)


def coarse_everywhere(local, ids, factors):
    members = lax.axis_size("mem")
    slabs = lax.axis_size("grp")
    owned = NC // BS // members
    shares = slabs // owned
    sides = RHS // shares
    summed = jax.ops.segment_sum(local.T, ids, num_segments=NC)
    parts = summed.reshape(members, owned, BS, shares, sides).transpose(1, 3, 0, 4, 2)
    parts = parts.reshape(slabs * members, sides, BS)
    pieces = lax.all_to_all(parts, BOTH, 0, 0, tiled=True)
    mine = jnp.sum(pieces, axis=0)
    factor = lax.dynamic_index_in_dim(factors, lax.axis_index("grp") // shares, 0, keepdims=False)
    inner = jnp.einsum("kj,ij->ki", mine, factor, precision=lax.Precision.HIGHEST)
    fix = jnp.einsum("ki,ij->kj", inner, factor, precision=lax.Precision.HIGHEST)
    copies = jnp.broadcast_to(fix, (slabs * members, *fix.shape))
    fixes = lax.all_to_all(copies, BOTH, 0, 0, tiled=True)
    fixes = fixes.reshape(owned, shares, members, sides, BS).transpose(1, 3, 2, 0, 4)
    return jnp.take(fixes.reshape(RHS, NC), ids, axis=1)


def shards(forcing, aggregate, factors):
    slab, member = lax.axis_index("grp"), lax.axis_index("mem")
    slabs, members = lax.axis_size("grp"), lax.axis_size("mem")

    def place_of(index, size):
        return jnp.where(index == 0, 1, jnp.where(index == size - 1, 2, 0))

    place = (place_of(slab, slabs) * 3 + place_of(member, members)).reshape(1).astype(jnp.int32)
    inside = jnp.stack([slab > 0, slab < slabs - 1, member > 0, member < members - 1])
    inside = inside.astype(jnp.int32)

    ids = with_rim(with_rim(aggregate, "grp", 0, 1), "mem", 1, 1).reshape(-1)
    ylo, yhi = rim_of(forcing, "mem", 2, RIM)
    local = restrict_own(forcing, place)
    local = local.reshape(GROUPS, RHS, NZ).transpose(1, 0, 2).reshape(RHS, GROUPS * NZ)
    picked = coarse_everywhere(local, ids, factors)
    coarse = picked.reshape(RHS, GROUPS, NZ).transpose(1, 0, 2).reshape(GROUPS * RHS, NZ)

    def edge(at):
        return jnp.concatenate(
            [lax.slice_in_dim(v, at, at + RIM, axis=1) for v in (ylo, forcing, yhi)], axis=2
        )

    up, down = shift_pairs(slabs)
    xlo = lax.ppermute(edge(SIDE - RIM), "grp", up)
    xhi = lax.ppermute(edge(0), "grp", down)
    smooth = smooth_all(forcing, ylo, yhi, xlo, xhi, inside)
    return add_correction(smooth, coarse, place)


def solution(mesh):
    placed = (P(None, "grp", "mem", None), P("grp", "mem", None), P("mem", None, None))
    return jax.shard_map(
        shards, mesh=mesh, in_specs=placed, out_specs=P(None, "grp", "mem", None), check_vma=False
    )
```

time: 285 us -> 137 us (0.48); the launches traced: 282 us -> 137 us
  blocking collectives: 77.7 us -> 0 us
  local copies, waits for them, and re-layouts: 59.9 us -> 20.8 us
  other arithmetic: 38.3 us -> 14.2 us
  starting transfers between devices: 76.7 us -> 53.8 us
  Pallas kernels: 0 us -> 20.9 us
    all_to_all x2 -> x0, blocking collectives: 77.7 us -> none  [the longest x1 63.7 us: from_everyone(): return lax.all_to_all(copies, axis, split_axis=0, concat_axis=0, tiled=True)]
    ppermute x24 -> x8, starting transfers between devices: 72.9 us -> 26.5 us  [the longest x3 15.2 us: rim_of(): lax.ppermute(lax.slice_in_dim(value, length - width, length, axis=dim), a...]
    all_to_all x1 -> x2, starting transfers between devices: 3.78 us -> 27.3 us  [the longest x1 15.8 us: coarse_everywhere(): pieces = lax.all_to_all(parts, BOTH, 0, 0, tiled=True)]
    pallas_call x0 -> x3, Pallas kernels: none -> 20.9 us  [the longest x1 12.4 us: smooth_all(): pl.pallas_call(smooth_kernel, out_shape=jax.ShapeDtypeStruct(forcing.shap...]
    slice x22 -> x6, local copies, waits for them, and re-layouts: 22.7 us -> 6.57 us  [the longest x2 3.3 us: rim_of(): high = lax.ppermute(lax.slice_in_dim(value, 0, width, axis=dim), axis, down)]
    add x5 -> x0, other arithmetic: 15.7 us -> none  [the longest x2 8.77 us: shards(): smoothed = smoothed + weight * (forcing - apply_operator(smoothed))]
    ppermute x24 -> x8, waiting for transfers between devices: 18.3 us -> 6.14 us  [the longest x3 6.13 us: rim_of(): high = lax.ppermute(lax.slice_in_dim(value, 0, width, axis=dim), axis, down)]
    reduce_sum x3 -> x1, other arithmetic: 12.2 us -> 0.28 us  [coarse_everywhere(): mine = jnp.sum(pieces, axis=0)]
  transfers between devices with their start and end apart: 25 -> 10, of which waited for: 7 -> 3; matrix products, arithmetic and copies ran while one was open for 5% -> 19% of each run, Pallas kernels for 0% -> 12%
where the time goes in v1:
time: 137 us
  starting transfers between devices  53.8 us (39%)
  waiting for transfers between devices  26.1 us (19%)
  Pallas kernels  20.9 us (15%)
  local copies, waits for them, and re-layouts  20.8 us (15%)
  other arithmetic  14.2 us (10%)
    all_to_all x1, starting transfers between devices, coarse_everywhere(): pieces = lax.all_to_all(parts, BOTH, 0, 0, tiled=True)  15.8 us
    ppermute x3, starting transfers between devices, rim_of(): lax.ppermute(lax.slice_in_dim(value, length - width, length, axis=dim), a...  15.2 us
    pallas_call x1, Pallas kernels, smooth_all(): pl.pallas_call(smooth_kernel, out_shape=jax.ShapeDtypeStruct(forcing.shap...  12.4 us
    all_to_all x1, starting transfers between devices, coarse_everywhere(): fixes = lax.all_to_all(copies, BOTH, 0, 0, tiled=True)  11.5 us
    scatter-add x1, other arithmetic, coarse_everywhere(): summed = jax.ops.segment_sum(local.T, ids, num_segments=NC)  11.4 us
    all_to_all x1, waiting for transfers between devices, coarse_everywhere(): pieces = lax.all_to_all(parts, BOTH, 0, 0, tiled=True)  11.3 us
    all_to_all x1, waiting for transfers between devices, coarse_everywhere(): fixes = lax.all_to_all(copies, BOTH, 0, 0, tiled=True)  8.68 us
    ppermute x3, waiting for transfers between devices, rim_of(): high = lax.ppermute(lax.slice_in_dim(value, 0, width, axis=dim), axis, down)  6.13 us
  transfers between devices with their start and end apart: 10, of which 3 were waited for; matrix products, arithmetic and copies ran while one was open for 19% of the time, Pallas kernels for 12%

profile of v1, /device:TPU:1, one launch (start us, length us, event | category | flops | bytes accessed | tf_op | source)
XLA Modules:
  0.0 136.6 jit_solution(3057828804623158624)
XLA Ops:
  0.0 0.8 fusion.16
  0.8 6.3 %collective-permute-start = (s32[1,4,32]{2,1,0:T(4,128)S(1)}, s32[1,4,32]{2,1,0:T(4,128)S(1)}, u32[]{:S(2)}, u32[]{:S(2)}) collective-permute-start(s32[1,4,32]{2,1,0:T(4,128)S(1)} %get-tuple-element.16), channel_id=1, source_target_pairs={{0,8},{8,16},{16,24},{24,32},{32,40},{40,48},{48,56},{56,64},{64,7... | collective-permute-start | bytes 1544 | tf_op jit(solution)/shard_map/ppermute | solution.py:282
  7.0 1.9 %collective-permute-start.1 = (s32[1,4,32]{2,1,0:T(4,128)S(1)}, s32[1,4,32]{2,1,0:T(4,128)S(1)}, u32[]{:S(2)}, u32[]{:S(2)}) collective-permute-start(s32[1,4,32]{2,1,0:T(4,128)S(1)} %get-tuple-element.15), channel_id=1, source_target_pairs={{8,0},{16,8},{24,16},{32,24},{40,32},{48,40},{56,48},{64,56},{72,6... | collective-permute-start | bytes 1544 | tf_op jit(solution)/shard_map/ppermute | solution.py:283
  9.0 2.5 %fusion.12 = (f32[16,16,4,128]{3,2,1,0:T(4,128)}, f32[16,16,4,128]{3,2,1,0:T(4,128)S(1)}) fusion(f32[16,16,16,128]{3,2,1,0:T(8,128)} %f_ref.3), kind=kLoop, calls=%fused_computation.26 | loop fusion | bytes 2097152 | tf_op jit(solution)/shard_map/slice | solution.py:283
  11.5 4.4 %collective-permute-start.4 = (f32[16,16,4,128]{3,2,1,0:T(4,128)S(1)}, f32[16,16,4,128]{3,2,1,0:T(4,128)}, u32[]{:S(2)}, u32[]{:S(2)}) collective-permute-start(f32[16,16,4,128]{3,2,1,0:T(4,128)S(1)} %get-tuple-element.8), channel_id=1, source_target_pairs={{0,1},{1,2},{2,3},{3,4},{4,5},{5,6},{6,7},{8,9},{9,10},{10,11},{11... | collective-permute-start | bytes 1572872 | tf_op jit(solution)/shard_map/ppermute | solution.py:282
  15.9 1.3 collective-permute-start.5
  17.2 1.3 fusion.11
  18.5 0.0 copy-start.1
  18.5 3.8 %restrict.1 = f32[144,128]{1,0:T(8,128)} custom-call(s32[1]{0:T(128)} %bitcast.place_ref, f32[16,16,16,128]{3,2,1,0:T(8,128)} %f_ref.3, bf16[9,2,144,256]{3,2,1,0:T(8,128)(2,1)} %constant.62.clone.plane_ref, bf16[2,512,128]{2,1,0:T(8,128)(2,1)} %constant.63.clone.line_ref), custom_call_target="tpu_custom_call" | custom-call | flops 6000000000 | bytes 3145728 | tf_op jit(solution)/shard_map/restrict/pallas_call | solution.py:132
  22.3 0.7 add_convert_fusion.inside_ref
  23.0 1.1 copy.15
  24.2 1.3 collective-permute-start.3
  25.5 4.6 %collective-permute-start.2 = (s32[6,1,32]{2,1,0:T(1,128)S(1)}, s32[6,1,32]{2,1,0:T(1,128)S(1)}, u32[]{:S(2)}, u32[]{:S(2)}) collective-permute-start(s32[6,1,32]{2,1,0:T(1,128)S(1)} %get-tuple-element.13), channel_id=1, source_target_pairs={{0,1},{1,2},{2,3},{3,4},{4,5},{5,6},{6,7},{8,9},{9,10},{10,11},{11... | collective-permute-start | bytes 2312 | tf_op jit(solution)/shard_map/ppermute | solution.py:282
  30.1 6.1 %collective-permute-done.3 = s32[6,1,32]{2,1,0:T(1,128)S(1)} collective-permute-done((s32[6,1,32]{2,1,0:T(1,128)S(1)}, s32[6,1,32]{2,1,0:T(1,128)S(1)}, u32[]{:S(2)}, u32[]{:S(2)}) %collective-permute-start.3) | collective-permute-done | bytes 800 | tf_op jit(solution)/shard_map/ppermute | solution.py:283
  36.2 0.0 collective-permute-done.2
  36.3 0.1 reshape.87
  36.3 0.1 broadcast_in_dim_reshape.3
  36.4 11.4 %scatter_custom_fusion = f32[8192,16]{1,0:T(8,128)} fusion(s32[1152]{0:T(1024)S(1)} %reshape.87, f32[1152,16]{1,0:T(8,128)S(1)} %bitcast.42, f32[]{:T(128)} %constant.58.clone.1), kind=kCustom, calls=%fused_computation.2 | custom fusion | flops 18432 | bytes 524292 | tf_op jit(solution)/shard_map/scatter-add | solution.py:298
  47.8 2.8 %copy.16 = f32[8192,16]{0,1:T(8,128)S(1)} copy(f32[8192,16]{1,0:T(8,128)} %scatter_custom_fusion) | data formatting | bytes 1048576 | tf_op jit(solution)/shard_map/scatter-add | solution.py:298
  50.6 0.1 copy.23
  50.7 0.1 copy.17
  50.9 1.1 copy.18
  52.0 15.8 %all-to-all-start = ((f32[256,4,128]{2,1,0:T(4,128)}), f32[256,4,128]{2,1,0:T(4,128)S(1)}, u32[]{:S(2)}, u32[]{:S(2)}) async-start(f32[256,4,128]{2,1,0:T(4,128)} %copy.18), calls=%async_computation | async-start | bytes 1048576 | tf_op jit(solution)/shard_map/all_to_all | solution.py:301
  67.8 0.0 collective-permute-done.5.yhi_ref
  67.8 1.0 fusion.14
  68.8 0.0 collective-permute-done.4.ylo_ref
  68.8 1.0 fusion.13
  69.8 0.1 pad_maximum_fusion
  69.9 4.8 %collective-permute-start.6 = (f32[16,4,24,128]{3,2,1,0:T(8,128)S(1)}, f32[16,4,24,128]{3,2,1,0:T(8,128)}, u32[]{:S(2)}, u32[]{:S(2)}) collective-permute-start(f32[16,4,24,128]{3,2,1,0:T(8,128)S(1)} %pad_maximum_fusion), channel_id=1, source_target_pairs={{0,8},{8,16},{16,24},{24,32},{32,40},{40,48},{48,56},{56,64},{64,7... | collective-permute-start | bytes 2359304 | tf_op jit(solution)/shard_map/ppermute | solution.py:336
  74.8 1.0 pad_maximum_fusion.1
  75.8 1.9 %collective-permute-start.7 = (f32[16,4,24,128]{3,2,1,0:T(8,128)}, f32[16,4,24,128]{3,2,1,0:T(8,128)}, u32[]{:S(2)}, u32[]{:S(2)}) collective-permute-start(f32[16,4,24,128]{3,2,1,0:T(8,128)} %pad_maximum_fusion.1), channel_id=1, source_target_pairs={{8,0},{16,8},{24,16},{32,24},{40,32},{48,40},{56,48},{64,56},{72,6... | collective-permute-start | bytes 2359304 | tf_op jit(solution)/shard_map/ppermute | solution.py:337
  77.7 0.1 reshape.69
  77.8 11.3 %all-to-all-done = f32[256,4,128]{2,1,0:T(4,128)S(1)} async-done(((f32[256,4,128]{2,1,0:T(4,128)}), f32[256,4,128]{2,1,0:T(4,128)S(1)}, u32[]{:S(2)}, u32[]{:S(2)}) %all-to-all-start) | async-done | bytes 524320 | tf_op jit(solution)/shard_map/all_to_all | solution.py:301
  89.1 0.3 reduce_sum.9
  89.4 0.2 fusion.4
  89.6 0.2 fusion.2
  89.8 0.9 broadcast_in_dim.18
  90.7 11.5 %all-to-all-start.1 = ((f32[256,4,128]{2,1,0:T(4,128)}), f32[256,4,128]{2,1,0:T(4,128)S(1)}, u32[]{:S(2)}, u32[]{:S(2)}) async-start(f32[256,4,128]{2,1,0:T(4,128)} %broadcast_in_dim.18), calls=%async_computation.1 | async-start | bytes 1048576 | tf_op jit(solution)/shard_map/all_to_all | solution.py:307
  102.3 0.0 collective-permute-done.6.xlo_ref
  102.3 12.4 %smooth.1.q_ref = f32[16,16,16,128]{3,2,1,0:T(8,128)} custom-call(s32[4]{0:T(128)} %add_convert_fusion.inside_ref, f32[16,16,16,128]{3,2,1,0:T(8,128)} %f_ref.3, f32[16,16,4,128]{3,2,1,0:T(4,128)} %collective-permute-done.4.ylo_ref, f32[16,16,4,128]{3,2,1,0:T(4,128)} %collective-permute-done.5.yhi_ref, f32[16,4,24,128]{3,2,1,0:T(8,128)} %collective-permute-done.6.xlo_ref, ...), custom_call_target="tpu_custom_call" | custom-call | flops 10000000000 | bytes 7340032 | tf_op jit(solution)/shard_map/smooth/pallas_call | solution.py:257
  114.7 8.7 %all-to-all-done.1 = f32[256,4,128]{2,1,0:T(4,128)S(1)} async-done(((f32[256,4,128]{2,1,0:T(4,128)}), f32[256,4,128]{2,1,0:T(4,128)S(1)}, u32[]{:S(2)}, u32[]{:S(2)}) %all-to-all-start.1) | async-done | bytes 524320 | tf_op jit(solution)/shard_map/all_to_all | solution.py:307
  123.4 0.3 copy.20
  123.7 0.1 reshape.75
  123.8 2.6 %copy.21 = f32[16,8192]{0,1:T(8,128)} copy(f32[16,8192]{1,0:T(8,128)S(1)} %reshape.75) | data formatting | bytes 1048576 | tf_op jit(solution)/shard_map/reshape | solution.py:309
  126.5 4.6 %gather_fusion = f32[1152,16]{1,0:T(8,128)S(1)} fusion(f32[16,8192]{0,1:T(8,128)} %copy.21, s32[2048]{0:T(1024)S(1)} %pad_clamp_fusion), kind=kCustom, calls=%fused_computation | custom fusion | bytes 152064 | tf_op jit(solution)/shard_map/jit(_take)/gather | solution.py:309
  131.1 0.2 copy.22
  131.3 0.7 broadcast_select_fusion
  131.9 4.7 %correct.1 = f32[16,16,16,128]{3,2,1,0:T(8,128)} custom-call(s32[1]{0:T(128)} %bitcast.place_ref, f32[144,128]{1,0:T(8,128)} %bitcast.43, f32[16,16,16,128]{3,2,1,0:T(8,128)} %smooth.1.q_ref, bf16[9,2,144,256]{3,2,1,0:T(8,128)(2,1)} %constant.62.clone.plane_ref, bf16[2,128,512]{2,1,0:T(8,128)(2,1)} %constant.64.clone.line_ref), custom_call_target="tpu_custom_call" | custom-call | flops 6000000000 | bytes 5242880 | tf_op jit(solution)/shard_map/correct/pallas_call | solution.py:175
  (15 shorter events, 0.1 us)
Async XLA Ops:
  0.0 89.4 %copy-start = (f32[8,128,128]{2,1,0:T(8,128)S(1)}, f32[8,128,128]{2,1,0:T(8,128)}, u32[]{:S(2)}) copy-start(f32[8,128,128]{2,1,0:T(8,128)} %param.8) | copy-start | bytes 1572868
  0.8 23.3 %collective-permute-start = (s32[1,4,32]{2,1,0:T(4,128)S(1)}, s32[1,4,32]{2,1,0:T(4,128)S(1)}, u32[]{:S(2)}, u32[]{:S(2)}) collective-permute-start(s32[1,4,32]{2,1,0:T(4,128)S(1)} %get-tuple-element.16), channel_id=1, source_target_pairs={{0,8},{8,16},{16,24},{24,32},{32,40},{40,48},{48,56},{56,64},{64,7... | collective-permute-start | bytes 1544 | tf_op jit(solution)/shard_map/ppermute | solution.py:282
  7.0 17.1 %collective-permute-start.1 = (s32[1,4,32]{2,1,0:T(4,128)S(1)}, s32[1,4,32]{2,1,0:T(4,128)S(1)}, u32[]{:S(2)}, u32[]{:S(2)}) collective-permute-start(s32[1,4,32]{2,1,0:T(4,128)S(1)} %get-tuple-element.15), channel_id=1, source_target_pairs={{8,0},{16,8},{24,16},{32,24},{40,32},{48,40},{56,48},{64,56},{72,6... | collective-permute-start | bytes 1544 | tf_op jit(solution)/shard_map/ppermute | solution.py:283
  11.5 57.3 %collective-permute-start.4 = (f32[16,16,4,128]{3,2,1,0:T(4,128)S(1)}, f32[16,16,4,128]{3,2,1,0:T(4,128)}, u32[]{:S(2)}, u32[]{:S(2)}) collective-permute-start(f32[16,16,4,128]{3,2,1,0:T(4,128)S(1)} %get-tuple-element.8), channel_id=1, source_target_pairs={{0,1},{1,2},{2,3},{3,4},{4,5},{5,6},{6,7},{8,9},{9,10},{10,11},{11... | collective-permute-start | bytes 1572872 | tf_op jit(solution)/shard_map/ppermute | solution.py:282
  15.9 51.9 %collective-permute-start.5 = (f32[16,16,4,128]{3,2,1,0:T(4,128)}, f32[16,16,4,128]{3,2,1,0:T(4,128)}, u32[]{:S(2)}, u32[]{:S(2)}) collective-permute-start(f32[16,16,4,128]{3,2,1,0:T(4,128)} %get-tuple-element.7), channel_id=1, source_target_pairs={{1,0},{2,1},{3,2},{4,3},{5,4},{6,5},{7,6},{9,8},{10,9},{11,10},{12... | collective-permute-start | bytes 1572872 | tf_op jit(solution)/shard_map/ppermute | solution.py:283
  18.5 5.6 %copy-start.1 = (s32[4,4,32]{2,1,0:T(4,128)S(1)}, s32[4,4,32]{2,1,0:T(4,128)}, u32[]{:S(2)}) copy-start(s32[4,4,32]{2,1,0:T(4,128)} %param.7) | copy-start | bytes 6148
  24.2 12.1 %collective-permute-start.3 = (s32[6,1,32]{2,1,0:T(1,128)S(1)}, s32[6,1,32]{2,1,0:T(1,128)S(1)}, u32[]{:S(2)}, u32[]{:S(2)}) collective-permute-start(s32[6,1,32]{2,1,0:T(1,128)S(1)} %get-tuple-element.14), channel_id=1, source_target_pairs={{1,0},{2,1},{3,2},{4,3},{5,4},{6,5},{7,6},{9,8},{10,9},{11,10},{12... | collective-permute-start | bytes 2312 | tf_op jit(solution)/shard_map/ppermute | solution.py:283
  25.5 10.8 %collective-permute-start.2 = (s32[6,1,32]{2,1,0:T(1,128)S(1)}, s32[6,1,32]{2,1,0:T(1,128)S(1)}, u32[]{:S(2)}, u32[]{:S(2)}) collective-permute-start(s32[6,1,32]{2,1,0:T(1,128)S(1)} %get-tuple-element.13), channel_id=1, source_target_pairs={{0,1},{1,2},{2,3},{3,4},{4,5},{5,6},{6,7},{8,9},{9,10},{10,11},{11... | collective-permute-start | bytes 2312 | tf_op jit(solution)/shard_map/ppermute | solution.py:282
  52.0 37.1 %all-to-all-start = ((f32[256,4,128]{2,1,0:T(4,128)}), f32[256,4,128]{2,1,0:T(4,128)S(1)}, u32[]{:S(2)}, u32[]{:S(2)}) async-start(f32[256,4,128]{2,1,0:T(4,128)} %copy.18), calls=%async_computation | async-start | bytes 1048576 | tf_op jit(solution)/shard_map/all_to_all | solution.py:301
  69.9 32.3 %collective-permute-start.6 = (f32[16,4,24,128]{3,2,1,0:T(8,128)S(1)}, f32[16,4,24,128]{3,2,1,0:T(8,128)}, u32[]{:S(2)}, u32[]{:S(2)}) collective-permute-start(f32[16,4,24,128]{3,2,1,0:T(8,128)S(1)} %pad_maximum_fusion), channel_id=1, source_target_pairs={{0,8},{8,16},{16,24},{24,32},{32,40},{40,48},{48,56},{56,64},{64,7... | collective-permute-start | bytes 2359304 | tf_op jit(solution)/shard_map/ppermute | solution.py:336
  75.8 26.5 %collective-permute-start.7 = (f32[16,4,24,128]{3,2,1,0:T(8,128)}, f32[16,4,24,128]{3,2,1,0:T(8,128)}, u32[]{:S(2)}, u32[]{:S(2)}) collective-permute-start(f32[16,4,24,128]{3,2,1,0:T(8,128)} %pad_maximum_fusion.1), channel_id=1, source_target_pairs={{8,0},{16,8},{24,16},{32,24},{40,32},{48,40},{56,48},{64,56},{72,6... | collective-permute-start | bytes 2359304 | tf_op jit(solution)/shard_map/ppermute | solution.py:337
  90.7 32.7 %all-to-all-start.1 = ((f32[256,4,128]{2,1,0:T(4,128)}), f32[256,4,128]{2,1,0:T(4,128)S(1)}, u32[]{:S(2)}, u32[]{:S(2)}) async-start(f32[256,4,128]{2,1,0:T(4,128)} %broadcast_in_dim.18), calls=%async_computation.1 | async-start | bytes 1048576 | tf_op jit(solution)/shard_map/all_to_all | solution.py:307
